TPU v7x, 32 devices: a whole 2x2x4 slice. The times are simulated.
32 devices in a mesh: section: 4 (over x, core), dp: 8 (over z, y).
Axes of the slice: x: 2, y: 2, z: 4, core: 2. Of those that a mesh axis runs over, the one named last changes fastest.
Arguments:
- obs_features: bfloat16 [4, 256, 1024], P(None, 'dp'), may hold values from -1.1953125 to 1.1953125
- w_input: bfloat16 [4, 1024, 4096], P('section'), may hold values from -1 to 1
- w_recurrent: bfloat16 [4, 1024, 4096], P('section', None, 'dp'), may hold values from -0.1875 to 0.1875
- bias: float32 [4, 4096], P('section'), may hold values from -3 to 3
- stored_states: bfloat16 [4, 4, 256, 2048], P('section', None, 'dp'), may hold values from -3 to 3
- state_owner: int32 [256], P('dp'), may hold values from 0 to 3
- burn_steps: int32 [256], P('dp'), may hold values from 1 to 2
- valid_steps: int32 [256], P('dp'), may hold values from 3 to 4
- cotangent: bfloat16 [4, 256, 1024], P(None, 'dp'), may hold values from -3 to 3
Outputs:
- hidden_all: bfloat16 [4, 4, 256, 1024], P('section', None, 'dp')
- grad_recurrent: float32 [4, 1024, 4096], P('section', None, 'dp')
- grad_bias: float32 [4, 4096], P('section', 'dp')
All inputs are finite; a program needn't handle non-finite values.
Results may differ from a plain program's by a relative error of at most 0.017.
Values may be sent and summed in bfloat16 or wider, within the bound.
No kernel may reach another device: no remote copies, remote signals or barrier semaphores. Data moves between devices by JAX's collectives and lax.ppermute only.
A program may use at most 128 MiB of HBM per device.

v0:
```python
from functools import partial
import jax
import jax.numpy as jnp
from jax import lax
from jax.sharding import PartitionSpec as P


def from_behind(array, axis, by):
    peers = lax.axis_size(axis)
    pairs = [(i, i + by) for i in range(peers) if 0 <= i + by < peers]
    return lax.ppermute(array, axis, pairs)


def lstm_cell(preact, cell_prev):
    breadth = cell_prev.shape[-1]
    in_gate = jax.nn.sigmoid(preact[:, :breadth])
    forget = jax.nn.sigmoid(preact[:, breadth : 2 * breadth])
    candidate = jnp.tanh(preact[:, 2 * breadth : 3 * breadth])
    out_gate = jax.nn.sigmoid(preact[:, 3 * breadth :])
    cell_new = forget * cell_prev + in_gate * candidate
    hidden_new = (out_gate * jnp.tanh(cell_new)).astype(jnp.bfloat16)
    gate_vals = jnp.concatenate([in_gate, forget, candidate, out_gate], axis=-1)
    return (hidden_new, cell_new, gate_vals)


def forward_span(inputs, w_in, w_rec, bias_row, hidden_start, cell_start):
    step_count, seq_rows, breadth = inputs.shape
    projected = jnp.dot(
        inputs.reshape(step_count * seq_rows, breadth), w_in, preferred_element_type=jnp.float32
    )
    projected = projected.reshape(step_count, seq_rows, -1) + bias_row

    def advance(carried, proj_row):
        hidden_prev, cell_prev = carried
        preact = proj_row + jnp.dot(hidden_prev, w_rec, preferred_element_type=jnp.float32)
        hidden_new, cell_new, gate_vals = lstm_cell(preact, cell_prev)
        return ((hidden_new, cell_new), (hidden_new, cell_new, gate_vals))

    (hidden_end, cell_end), (hidden_seq, cell_seq, gate_seq) = lax.scan(
        advance, (hidden_start, cell_start), projected
    )
    return (hidden_seq, cell_seq, gate_seq, hidden_end, cell_end)


def times_transposed(operand, matrix):
    return lax.dot_general(
        operand, matrix, (((1,), (1,)), ((), ())), preferred_element_type=jnp.float32
    )


def backward_span(above_grads, cell_now, cell_old, gate_seq, live_mask, w_rec, grad_h, grad_c):

    def retreat(carried, inputs):
        grad_hidden, grad_cell = carried
        grad_out, cell_cur, cell_before, gate_vals, alive_row = inputs
        breadth = cell_cur.shape[-1]
        in_gate = gate_vals[:, :breadth]
        forget = gate_vals[:, breadth : 2 * breadth]
        candidate = gate_vals[:, 2 * breadth : 3 * breadth]
        out_gate = gate_vals[:, 3 * breadth :]
        total_h = grad_out.astype(jnp.float32) + grad_hidden
        squashed = jnp.tanh(cell_cur)
        total_c = grad_cell + total_h * out_gate * (1.0 - squashed * squashed)
        grad_pre = (
            jnp.concatenate(
                [
                    total_c * candidate * in_gate * (1.0 - in_gate),
                    total_c * cell_before * forget * (1.0 - forget),
                    total_c * in_gate * (1.0 - candidate * candidate),
                    total_h * squashed * out_gate * (1.0 - out_gate),
                ],
                axis=-1,
            )
            * alive_row[:, None]
        )
        gate_grads = grad_pre.astype(jnp.bfloat16)
        return (
            (times_transposed(gate_grads, w_rec), total_c * forget * alive_row[:, None]),
            gate_grads,
        )

    (grad_h_end, grad_c_end), gate_grads = lax.scan(
        retreat,
        (grad_h, grad_c),
        (above_grads, cell_now, cell_old, gate_seq, live_mask),
        reverse=True,
    )
    return (gate_grads, grad_h_end, grad_c_end)


def on_device(
    obs_features,
    w_input,
    w_recurrent,
    bias,
    stored_states,
    state_owner,
    burn_steps,
    valid_steps,
    cotangent,
):
    section_index = lax.axis_index("section")
    sections = lax.axis_size("section")
    step_count, seq_rows, breadth = obs_features.shape
    gate_width = 4 * breadth
    w_in = w_input[0]
    bias_row = bias[0]
    owned_rows = (state_owner == section_index)[None, :, None]
    state_table = jnp.where(owned_rows, stored_states[0].astype(jnp.float32), jnp.float32(0.0))
    delivered = lax.psum_scatter(
        state_table.astype(jnp.bfloat16), "section", scatter_dimension=0, tiled=True
    ).astype(jnp.float32)[0]
    hidden_start = delivered[:, :breadth].astype(jnp.bfloat16)
    cell_start = delivered[:, breadth:]
    w_rec = lax.all_gather(w_recurrent[0], "dp", axis=1, tiled=True)
    positions = jnp.arange(step_count, dtype=jnp.int32)[:, None]
    live_mask = ((positions >= burn_steps[None, :]) & (positions < valid_steps[None, :])).astype(
        jnp.float32
    )
    block_total = 1
    block_len = step_count // block_total
    tick_count = block_total + sections - 1

    def advance_block(inputs, offset, carried):
        hidden_now, cell_now, hidden_buf, cell_buf, gate_buf = carried
        hidden_seq, cell_seq, gate_seq, hidden_end, cell_end = forward_span(
            inputs, w_in, w_rec, bias_row, hidden_now, cell_now
        )
        hidden_buf = hidden_seq
        cell_buf = cell_seq
        gate_buf = gate_seq
        return ((hidden_end, cell_end, hidden_buf, cell_buf, gate_buf), hidden_seq)

    def keep_block(carried):
        return (carried, jnp.zeros((block_len, seq_rows, breadth), jnp.bfloat16))

    carried = (
        hidden_start,
        cell_start,
        jnp.zeros((step_count, seq_rows, breadth), jnp.bfloat16),
        jnp.zeros((step_count, seq_rows, breadth), jnp.float32),
        jnp.zeros((step_count, seq_rows, gate_width), jnp.float32),
    )
    incoming = jnp.zeros((block_len, seq_rows, breadth), jnp.bfloat16)
    for tick_index in range(tick_count):
        block_index = tick_index - section_index
        active = (block_index >= 0) & (block_index < block_total)
        offset = jnp.clip(block_index, 0, block_total - 1) * block_len
        inputs = jnp.where(section_index == 0, obs_features, incoming)
        carried, outgoing = lax.cond(
            active, partial(advance_block, inputs, offset), keep_block, carried
        )
        if tick_index + 1 < tick_count:
            incoming = from_behind(outgoing, "section", 1)
    hidden_buf = carried[2]
    cell_buf = carried[3]
    gate_buf = carried[4]
    cell_full = jnp.concatenate([cell_start[None], cell_buf], axis=0)

    def retreat_block(above_grads, offset, back_state):
        grad_h, grad_c, grad_buf = back_state
        cell_before = lax.dynamic_slice_in_dim(cell_full, offset, block_len, 0)
        gate_grads, grad_h, grad_c = backward_span(
            above_grads, cell_buf, cell_before, gate_buf, live_mask, w_rec, grad_h, grad_c
        )
        grad_buf = gate_grads

        def lower_input(values):
            return (
                times_transposed(values.reshape(-1, gate_width), w_in)
                .reshape(block_len, seq_rows, breadth)
                .astype(jnp.bfloat16)
            )

        def no_input(values):
            return jnp.zeros((block_len, seq_rows, breadth), jnp.bfloat16)

        lower_grads = lax.cond(section_index > 0, lower_input, no_input, gate_grads)
        return ((grad_h, grad_c, grad_buf), lower_grads)

    def keep_back(back_state):
        return (back_state, jnp.zeros((block_len, seq_rows, breadth), jnp.bfloat16))

    back_state = (
        jnp.zeros((seq_rows, breadth), jnp.float32),
        jnp.zeros((seq_rows, breadth), jnp.float32),
        jnp.zeros((step_count, seq_rows, gate_width), jnp.bfloat16),
    )
    arriving = jnp.zeros((block_len, seq_rows, breadth), jnp.bfloat16)
    for tick_index in range(tick_count):
        block_index = block_total - 1 - (tick_index - (sections - 1 - section_index))
        active = (block_index >= 0) & (block_index < block_total)
        offset = jnp.clip(block_index, 0, block_total - 1) * block_len
        above_grads = jnp.where(section_index == sections - 1, cotangent, arriving)
        back_state, sending = lax.cond(
            active, partial(retreat_block, above_grads, offset), keep_back, back_state
        )
        if tick_index + 1 < tick_count:
            arriving = from_behind(sending, "section", -1)
    gate_rows = back_state[2].reshape(step_count * seq_rows, gate_width)
    prev_rows = jnp.concatenate([hidden_start[None], hidden_buf[:-1]], axis=0).reshape(
        step_count * seq_rows, breadth
    )
    grad_cols = lax.all_to_all(gate_rows, "dp", split_axis=1, concat_axis=0, tiled=True)
    weight_grad = lax.dot_general(
        lax.all_gather(prev_rows, "dp", axis=0, tiled=True),
        grad_cols,
        (((0,), (0,)), ((), ())),
        preferred_element_type=jnp.float32,
    )
    bias_grad = jnp.sum(grad_cols, axis=0, dtype=jnp.float32)
    return (hidden_buf[None], weight_grad[None], bias_grad[None])


def solution(mesh):
    in_specs = (
        P(None, "dp", None),
        P("section", None, None),
        P("section", None, "dp"),
        P("section", None),
        P("section", None, "dp", None),
        P("dp"),
        P("dp"),
        P("dp"),
        P(None, "dp", None),
    )
    out_specs = (P("section", None, "dp", None), P("section", None, "dp"), P("section", "dp"))
    return jax.shard_map(
        on_device, mesh=mesh, in_specs=in_specs, out_specs=out_specs, check_vma=False
    )
```

profile of v0, /device:TPU:0, one launch (start us, length us, event | category | flops | bytes accessed | tf_op | source)
XLA Modules:
  0.0 535.3 jit_solution(6151085582079981420)
XLA Ops:
  8.8 2.0 fusion.141
  11.5 24.8 %reduce-scatter.2.cloned.1.call-done = bf16[1,32,2048]{2,1,0:T(8,128)(2,1)} async-done(((bf16[4,32,2048]{2,1,0:T(8,128)(2,1)}), bf16[1,32,2048]{2,1,0:T(8,128)(2,1)}) %reduce-scatter.2.cloned.1.call-update) | async-done | bytes 131088 | tf_op jit(solution)/shard_map/reduce_scatter | solution.py:110
  37.2 103.6 %all-gather.6.cloned.1.call-done = bf16[1,1024,4096]{2,1,0:T(8,128)(2,1)} async-done(((bf16[1,1024,512]{2,1,0:T(8,128)(2,1)}), bf16[1,1024,4096]{2,1,0:T(8,128)(2,1)}) %all-gather.6.cloned.1.call-update) | async-done | bytes 8388624 | tf_op jit(solution)/shard_map/all_gather | solution.py:115
  140.8 34.2 %conditional.11 = (bf16[32,1024]{1,0:T(8,128)(2,1)S(1)}, f32[32,1024]{1,0:T(8,128)S(1)}, bf16[4,32,1024]{2,1,0:T(8,128)(2,1)}, f32[4,32,1024]{2,1,0:T(8,128)}, f32[4,32,4096]{2,1,0:T(8,128)}) conditional(s32[]{:T(128)} %convert_element_type.215, (bf16[32,1024]{1,0:T(8,128)(2,1)S(1)}, f32[32,1024]{1,0:T(8,128)S(1)}) %tuple.195, ...), branch_computations={%region_1.2_spmd, %region_2.5_spmd} | conditional | flops 1343979520 | bytes 23545560 | solution.py:150
  140.8 4.6 fusion.12
  145.5 29.5 %while.150 = (s32[]{:T(128)}, bf16[32,1024]{1,0:T(8,128)(2,1)S(1)}, f32[32,1024]{1,0:T(8,128)S(1)}, bf16[4,32,1024]{2,1,0:T(8,128)(2,1)}, f32[4,32,1024]{2,1,0:T...) while((s32[]{:T(128)}, bf16[32,1024]{1,0:T(8,128)(2,1)S(1)}, ...), condition=%wide.region_4.4_spmd, body=%wide.region_3.3_spmd.sunk | while | flops 269713408 | bytes 12781153 | solution.py:39
  145.5 4.9 convolution_add_fusion.11
  152.9 4.9 convolution_add_fusion.11
  160.2 4.9 convolution_add_fusion.11
  167.6 4.9 convolution_add_fusion.11
  175.0 1.3 collective-permute-start
  176.3 1.3 collective-permute-done
  177.7 37.4 %collective-permute-start.1 = (bf16[4,32,1024]{2,1,0:T(8,128)(2,1)S(1)}, bf16[4,32,1024]{2,1,0:T(8,128)(2,1)S(1)}, u32[]{:S(2)}, u32[]{:S(2)}) collective-permute-start(bf16[4,32,1024]{2,1,0:T(8,128)(2,1)S(1)} %get-tuple-element.1425), channel_id=1, source_target_pairs={{0,8},{8,16},{16,24},{1,9},{9,17},{17,25},{2,10},{10,18},{18,26},{... | collective-permute-start | bytes 786440 | tf_op jit(solution)/shard_map/ppermute | solution.py:11
  216.3 4.1 collective-permute-start.2
  224.5 3.2 conditional.15
  227.7 1.3 collective-permute-start.3
  229.0 41.6 %collective-permute-done.3 = bf16[4,32,1024]{2,1,0:T(8,128)(2,1)S(1)} collective-permute-done((bf16[4,32,1024]{2,1,0:T(8,128)(2,1)}, bf16[4,32,1024]{2,1,0:T(8,128)(2,1)S(1)}, u32[]{:S(2)}, u32[]{:S(2)}) %collective-permute-start.3) | collective-permute-done | bytes 262176 | tf_op jit(solution)/shard_map/ppermute | solution.py:11
  272.6 7.3 %collective-permute-done.4 = bf16[4,32,1024]{2,1,0:T(8,128)(2,1)S(1)} collective-permute-done((bf16[4,32,1024]{2,1,0:T(8,128)(2,1)}, bf16[4,32,1024]{2,1,0:T(8,128)(2,1)S(1)}, u32[]{:S(2)}, u32[]{:S(2)}) %collective-permute-start.4) | collective-permute-done | bytes 262176 | tf_op jit(solution)/shard_map/ppermute | solution.py:11
  281.9 177.6 %collective-permute-done.5 = bf16[4,32,1024]{2,1,0:T(8,128)(2,1)S(1)} collective-permute-done((bf16[4,32,1024]{2,1,0:T(8,128)(2,1)}, bf16[4,32,1024]{2,1,0:T(8,128)(2,1)S(1)}, u32[]{:S(2)}, u32[]{:S(2)}) %collective-permute-start.5) | collective-permute-done | bytes 262176 | tf_op jit(solution)/shard_map/ppermute | solution.py:11
  459.5 42.7 %conditional.18 = (bf16[4,32,4096]{2,1,0:T(8,128)(2,1)}) conditional(s32[]{:T(128)} %convert_element_type.215, bf16[4,32,4096]{2,1,0:T(8,128)(2,1)} %get-tuple-element.1443, (pred[4,32,1024]{2,1,0:T(8,128)(4,1)S(1)}, bf16[4,32,1024]{2,1,0:T(8,128)(2,1)S(1)}, bf16[4,32,1024]{2,1,0:T(8,128)(2,1)S(1)}, s32[]{:T(128)}, f32[5,32,1024]{2,1,0:T(8,128)S(1)}, ...), branch_computations={%region_35.36_spmd, %region_36.39_spmd} | conditional | flops 270696448 | bytes 16057297 | solution.py:195
  460.8 41.5 %while.156 = (s32[]{:T(128)}, f32[32,1024]{1,0:T(8,128)}, f32[32,1024]{1,0:T(8,128)}, bf16[4,32,4096]{2,1,0:T(8,128)(2,1)}, bf16[4,32,1024]{2,1,0:T(8,128)(2,1)S...) while((s32[]{:T(128)}, f32[32,1024]{1,0:T(8,128)}, ...), condition=%wide.region_38.38_spmd, body=%wide.region_37.37_spmd.sunk | while | flops 270565376 | bytes 13042453 | solution.py:82
  461.9 1.8 multiply_multiply_fusion.8
  464.5 6.6 %fusion.206 = f32[32,1024]{1,0:T(8,128)} fusion(bf16[1024,4096]{1,0:T(8,128)(2,1)} %get-tuple-element.2300, f32[32,1024]{1,0:T(8,128)S(1)} %get-tuple-element.2149, f32[32,1024]{1,0:T(8,128)S(1)} %get-tuple-element.2151, f32[32,1024]{1,0:T(8,128)S(1)} %get-tuple-element.2152, f32[32,1024]{1,0:T(8,128)S(1)} %get-tuple-element.2153, f32[32]{0:T(128)S(1)} %fusion.205), kind=kOutput, calls=%fused_computation.162.clone.1 | convolution fusion | flops 269090816 | bytes 9044096 | tf_op jit(solution)/shard_map/cond/branch_1_fun/while/body/eval_jaxpr/dot_general | solution.py:46
  472.2 1.8 multiply_multiply_fusion.8
  474.8 6.6 %fusion.206 = f32[32,1024]{1,0:T(8,128)} fusion(bf16[1024,4096]{1,0:T(8,128)(2,1)} %get-tuple-element.2300, f32[32,1024]{1,0:T(8,128)S(1)} %get-tuple-element.2149, f32[32,1024]{1,0:T(8,128)S(1)} %get-tuple-element.2151, f32[32,1024]{1,0:T(8,128)S(1)} %get-tuple-element.2152, f32[32,1024]{1,0:T(8,128)S(1)} %get-tuple-element.2153, f32[32]{0:T(128)S(1)} %fusion.205), kind=kOutput, calls=%fused_computation.162.clone.1 | convolution fusion | flops 269090816 | bytes 9044096 | tf_op jit(solution)/shard_map/cond/branch_1_fun/while/body/eval_jaxpr/dot_general | solution.py:46
  482.6 1.8 multiply_multiply_fusion.8
  485.2 6.6 %fusion.206 = f32[32,1024]{1,0:T(8,128)} fusion(bf16[1024,4096]{1,0:T(8,128)(2,1)} %get-tuple-element.2300, f32[32,1024]{1,0:T(8,128)S(1)} %get-tuple-element.2149, f32[32,1024]{1,0:T(8,128)S(1)} %get-tuple-element.2151, f32[32,1024]{1,0:T(8,128)S(1)} %get-tuple-element.2152, f32[32,1024]{1,0:T(8,128)S(1)} %get-tuple-element.2153, f32[32]{0:T(128)S(1)} %fusion.205), kind=kOutput, calls=%fused_computation.162.clone.1 | convolution fusion | flops 269090816 | bytes 9044096 | tf_op jit(solution)/shard_map/cond/branch_1_fun/while/body/eval_jaxpr/dot_general | solution.py:46
  492.9 1.8 multiply_multiply_fusion.8
  495.6 6.6 %fusion.206 = f32[32,1024]{1,0:T(8,128)} fusion(bf16[1024,4096]{1,0:T(8,128)(2,1)} %get-tuple-element.2300, f32[32,1024]{1,0:T(8,128)S(1)} %get-tuple-element.2149, f32[32,1024]{1,0:T(8,128)S(1)} %get-tuple-element.2151, f32[32,1024]{1,0:T(8,128)S(1)} %get-tuple-element.2152, f32[32,1024]{1,0:T(8,128)S(1)} %get-tuple-element.2153, f32[32]{0:T(128)S(1)} %fusion.205), kind=kOutput, calls=%fused_computation.162.clone.1 | convolution fusion | flops 269090816 | bytes 9044096 | tf_op jit(solution)/shard_map/cond/branch_1_fun/while/body/eval_jaxpr/dot_general | solution.py:46
  502.2 1.6 copy.14
  504.2 18.7 %all_to_all.19 = bf16[128,8,512]{2,0,1:T(8,128)(2,1)S(1)} all-to-all(bf16[128,8,512]{2,0,1:T(8,128)(2,1)S(1)} %copy.13), channel_id=1, replica_groups=mesh['section'=4,'dp'=8] {'dp'}, dimensions={1} | all-to-all | bytes 2097152 | tf_op jit(solution)/shard_map/all_to_all | solution.py:204
  523.6 4.2 convolution_bitcast_fusion
  (84 shorter events, 37.1 us)
Async XLA Ops:
  8.0 3.4 copy-start
  8.0 132.8 %copy-start.2 = (f32[1,4096]{1,0:T(1,128)S(1)}, f32[1,4096]{1,0:T(1,128)}, u32[]{:S(2)}) copy-start(f32[1,4096]{1,0:T(1,128)} %param.50) | copy-start | bytes 49156
  8.0 28.3 %reduce-scatter.2.cloned.1.call-start = ((), (), s32[]{:S(2)}) async-start(), calls=%async_computation.2 | async-start | bytes 655360 | tf_op jit(solution)/shard_map/reduce_scatter | solution.py:110
  10.8 130.0 %all-gather.6.cloned.1.call-start = ((), (), s32[]{:S(2)}) async-start(), calls=%async_computation.4 | async-start | bytes 9437184 | tf_op jit(solution)/shard_map/all_gather | solution.py:115
  11.4 512.3 %all-gather.4.cloned.1.call-start = ((), (), s32[]{:S(2)}) async-start(), calls=%async_computation.3 | async-start | bytes 2359296 | tf_op jit(solution)/shard_map/all_gather | solution.py:206
  175.0 2.6 collective-permute-start
  177.7 38.5 %collective-permute-start.1 = (bf16[4,32,1024]{2,1,0:T(8,128)(2,1)S(1)}, bf16[4,32,1024]{2,1,0:T(8,128)(2,1)S(1)}, u32[]{:S(2)}, u32[]{:S(2)}) collective-permute-start(bf16[4,32,1024]{2,1,0:T(8,128)(2,1)S(1)} %get-tuple-element.1425), channel_id=1, source_target_pairs={{0,8},{8,16},{16,24},{1,9},{9,17},{17,25},{2,10},{10,18},{18,26},{... | collective-permute-start | bytes 786440 | tf_op jit(solution)/shard_map/ppermute | solution.py:11
  216.3 5.2 collective-permute-start.2
  221.5 1.8 copy-start.3
  221.5 1.8 copy-start.4
  222.5 2.0 copy-start.1
  227.7 42.9 %collective-permute-start.3 = (bf16[4,32,1024]{2,1,0:T(8,128)(2,1)}, bf16[4,32,1024]{2,1,0:T(8,128)(2,1)S(1)}, u32[]{:S(2)}, u32[]{:S(2)}) collective-permute-start(bf16[4,32,1024]{2,1,0:T(8,128)(2,1)} %get-tuple-element.1438), channel_id=1, source_target_pairs={{8,0},{16,8},{24,16},{9,1},{17,9},{25,17},{10,2},{18,10},{26,18},{... | collective-permute-start | bytes 786440 | tf_op jit(solution)/shard_map/ppermute | solution.py:11
  271.3 8.6 %collective-permute-start.4 = (bf16[4,32,1024]{2,1,0:T(8,128)(2,1)}, bf16[4,32,1024]{2,1,0:T(8,128)(2,1)S(1)}, u32[]{:S(2)}, u32[]{:S(2)}) collective-permute-start(bf16[4,32,1024]{2,1,0:T(8,128)(2,1)} %get-tuple-element.1442), channel_id=1, source_target_pairs={{8,0},{16,8},{24,16},{9,1},{17,9},{25,17},{10,2},{18,10},{26,18},{... | collective-permute-start | bytes 786440 | tf_op jit(solution)/shard_map/ppermute | solution.py:11
  280.7 178.8 %collective-permute-start.5 = (bf16[4,32,1024]{2,1,0:T(8,128)(2,1)}, bf16[4,32,1024]{2,1,0:T(8,128)(2,1)S(1)}, u32[]{:S(2)}, u32[]{:S(2)}) collective-permute-start(bf16[4,32,1024]{2,1,0:T(8,128)(2,1)} %get-tuple-element.1444), channel_id=1, source_target_pairs={{8,0},{16,8},{24,16},{9,1},{17,9},{25,17},{10,2},{18,10},{26,18},{... | collective-permute-start | bytes 786440 | tf_op jit(solution)/shard_map/ppermute | solution.py:11
Sparse Core Ops, SparseCore 0:
  11.9 24.3 reduce-scatter.1
Sparse Core Ops, SparseCore 1:
  13.3 127.4 all-gather.5
  223.3 117.3 all-gather.3
where the time goes:
time: 536 us; the launch traced here: 535 us
  waiting for transfers between devices  359 us (67%)
  matrix products  55.1 us (10%)
  starting transfers between devices  46.8 us (9%)
  other arithmetic  26.7 us (5%)
  blocking collectives  18.7 us (3%)
  between operations  15.7 us (3%)
  local copies, waits for them, and re-layouts  13.2 us (2%)
    ppermute x6, waiting for transfers between devices, from_behind(): return lax.ppermute(array, axis, pairs)  230 us
    all_gather x1, waiting for transfers between devices, on_device(): w_rec = lax.all_gather(w_recurrent[0], 'dp', axis=1, tiled=True)  104 us
    ppermute x6, starting transfers between devices, from_behind(): return lax.ppermute(array, axis, pairs)  46.6 us
    dot_general x4, matrix products, times_transposed(): lax.dot_general(operand, matrix, (((1,), (1,)), ((), ())), preferred_elem...  26.6 us
    reduce_scatter x1, waiting for transfers between devices, on_device(): lax.psum_scatter(state_table.astype(jnp.bfloat16), 'section', scatter_dim...  24.8 us
    dot_general x4, matrix products, advance(): jnp.dot(hidden_prev, w_rec, preferred_element_type=jnp.float32)  19.7 us
    all_to_all x1, blocking collectives, on_device(): lax.all_to_all(gate_rows, 'dp', split_axis=1, concat_axis=0, tiled=True)  18.7 us
  transfers between devices with their start and end apart: 9, of which 8 were waited for; matrix products, arithmetic and copies ran while one was open for 10% of the time, Pallas kernels for 0%

commit v1 on v0

--- a/solution.py
+++ b/solution.py
@@ -112,7 +112,9 @@
     ).astype(jnp.float32)[0]
     hidden_start = delivered[:, :breadth].astype(jnp.bfloat16)
     cell_start = delivered[:, breadth:]
-    w_rec = lax.all_gather(w_recurrent[0], "dp", axis=1, tiled=True)
+    tile_in = w_recurrent[0]
+    tile_out = lax.all_gather(tile_in, "dp")
+    w_rec = jnp.concatenate(tile_out, axis=1)
     positions = jnp.arange(step_count, dtype=jnp.int32)[:, None]
     live_mask = ((positions >= burn_steps[None, :]) & (positions < valid_steps[None, :])).astype(
         jnp.float32

time: 536 us -> 642 us (1.20)
  waiting for transfers between devices: 359 us -> 417 us
  local copies, waits for them, and re-layouts: 13.2 us -> 48 us
  starting transfers between devices: 46.8 us -> 58.5 us
    ppermute x6, waiting for transfers between devices: 230 us -> 289 us  [from_behind(): return lax.ppermute(array, axis, pairs)]
    another operation x10 -> x12, local copies, waits for them, and re-layouts: 5.81 us -> 29.2 us
    ppermute x6, starting transfers between devices: 46.6 us -> 58.3 us  [from_behind(): return lax.ppermute(array, axis, pairs)]
    all_gather x0 -> x1, local copies, waits for them, and re-layouts: none -> 11.5 us  [on_device(): tile_out = lax.all_gather(tile_in, 'dp')]
where the time goes in v1:
time: 642 us; the launch traced here: 640 us
  waiting for transfers between devices  417 us (65%)
  starting transfers between devices  58.5 us (9%)
  matrix products  55.1 us (9%)
  local copies, waits for them, and re-layouts  48 us (7%)
  other arithmetic  26.7 us (4%)
  blocking collectives  18.6 us (3%)
  between operations  15.7 us (2%)
    ppermute x6, waiting for transfers between devices, from_behind(): return lax.ppermute(array, axis, pairs)  289 us
    all_gather x1, waiting for transfers between devices, on_device(): tile_out = lax.all_gather(tile_in, 'dp')  103 us
    ppermute x6, starting transfers between devices, from_behind(): return lax.ppermute(array, axis, pairs)  58.3 us
    another operation x12, local copies, waits for them, and re-layouts  29.2 us
    dot_general x4, matrix products, times_transposed(): lax.dot_general(operand, matrix, (((1,), (1,)), ((), ())), preferred_elem...  26.6 us
    reduce_scatter x1, waiting for transfers between devices, on_device(): lax.psum_scatter(state_table.astype(jnp.bfloat16), 'section', scatter_dim...  24.8 us
    dot_general x4, matrix products, advance(): jnp.dot(hidden_prev, w_rec, preferred_element_type=jnp.float32)  19.7 us
    all_to_all x1, blocking collectives, on_device(): lax.all_to_all(gate_rows, 'dp', split_axis=1, concat_axis=0, tiled=True)  18.6 us
  transfers between devices with their start and end apart: 9, of which 8 were waited for; matrix products, arithmetic and copies ran while one was open for 10% of the time, Pallas kernels for 0%

profile of v1, /device:TPU:0, one launch (start us, length us, event | category | flops | bytes accessed | tf_op | source)
XLA Modules:
  0.0 639.9 jit_solution(13734489165237088000)
XLA Ops:
  8.8 2.0 fusion.141
  11.5 24.8 %reduce-scatter.2.cloned.1.call-done = bf16[1,32,2048]{2,1,0:T(8,128)(2,1)} async-done(((bf16[4,32,2048]{2,1,0:T(8,128)(2,1)}), bf16[1,32,2048]{2,1,0:T(8,128)(2,1)}) %reduce-scatter.2.cloned.1.call-update) | async-done | bytes 131088 | tf_op jit(solution)/shard_map/reduce_scatter | solution.py:110
  37.2 103.1 %all-gather.3.cloned.1.call-done = bf16[8,1024,512]{2,1,0:T(8,128)(2,1)} async-done(((bf16[1,1024,512]{2,1,0:T(8,128)(2,1)}), bf16[8,1024,512]{2,1,0:T(8,128)(2,1)}) %all-gather.3.cloned.1.call-update) | async-done | bytes 8388624 | tf_op jit(solution)/shard_map/all_gather | solution.py:116
  140.3 11.5 %copy.17 = bf16[8,1024,512]{1,2,0:T(8,128)(2,1)} copy(bf16[8,1024,512]{2,1,0:T(8,128)(2,1)} %all-gather.3.cloned.1.call-done) | data formatting | bytes 16777216 | tf_op jit(solution)/shard_map/all_gather | solution.py:116
  151.8 45.9 %conditional.11 = (bf16[32,1024]{1,0:T(8,128)(2,1)S(1)}, f32[32,1024]{1,0:T(8,128)S(1)}, bf16[4,32,1024]{2,1,0:T(8,128)(2,1)}, f32[4,32,1024]{2,1,0:T(8,128)}, f32[4,32,4096]{2,1,0:T(8,128)}) conditional(s32[]{:T(128)} %convert_element_type.215, (bf16[32,1024]{1,0:T(8,128)(2,1)S(1)}, f32[32,1024]{1,0:T(8,128)S(1)}) %tuple.195, ...), branch_computations={%region_1.2_spmd, %region_2.5_spmd} | conditional | flops 1343979520 | bytes 40322776 | solution.py:152
  151.8 11.7 %copy.18 = bf16[1024,4096]{1,0:T(8,128)(2,1)} copy(bf16[1024,4096]{0,1:T(8,128)(2,1)} %get-tuple-element.1510) | data formatting | bytes 16777216 | tf_op jit(solution)/shard_map
  163.5 4.6 fusion.12
  168.2 29.5 %while.150 = (s32[]{:T(128)}, bf16[32,1024]{1,0:T(8,128)(2,1)S(1)}, f32[32,1024]{1,0:T(8,128)S(1)}, bf16[4,32,1024]{2,1,0:T(8,128)(2,1)}, f32[4,32,1024]{2,1,0:T...) while((s32[]{:T(128)}, bf16[32,1024]{1,0:T(8,128)(2,1)S(1)}, ...), condition=%wide.region_4.4_spmd, body=%wide.region_3.3_spmd.sunk | while | flops 269713408 | bytes 12781153 | solution.py:39
  168.2 4.9 convolution_add_fusion.11
  175.6 4.9 convolution_add_fusion.11
  182.9 4.9 convolution_add_fusion.11
  190.3 4.9 convolution_add_fusion.11
  200.4 49.1 %collective-permute-start.1 = (bf16[4,32,1024]{2,1,0:T(8,128)(2,1)S(1)}, bf16[4,32,1024]{2,1,0:T(8,128)(2,1)S(1)}, u32[]{:S(2)}, u32[]{:S(2)}) collective-permute-start(bf16[4,32,1024]{2,1,0:T(8,128)(2,1)S(1)} %get-tuple-element.1425), channel_id=1, source_target_pairs={{0,8},{8,16},{16,24},{1,9},{9,17},{17,25},{2,10},{10,18},{18,26},{... | collective-permute-start | bytes 786440 | tf_op jit(solution)/shard_map/ppermute | solution.py:11
  250.7 4.1 collective-permute-start.2
  258.9 3.2 conditional.15
  263.3 53.3 %collective-permute-done.3 = bf16[4,32,1024]{2,1,0:T(8,128)(2,1)S(1)} collective-permute-done((bf16[4,32,1024]{2,1,0:T(8,128)(2,1)}, bf16[4,32,1024]{2,1,0:T(8,128)(2,1)S(1)}, u32[]{:S(2)}, u32[]{:S(2)}) %collective-permute-start.3) | collective-permute-done | bytes 262176 | tf_op jit(solution)/shard_map/ppermute | solution.py:11
  318.7 7.3 %collective-permute-done.4 = bf16[4,32,1024]{2,1,0:T(8,128)(2,1)S(1)} collective-permute-done((bf16[4,32,1024]{2,1,0:T(8,128)(2,1)}, bf16[4,32,1024]{2,1,0:T(8,128)(2,1)S(1)}, u32[]{:S(2)}, u32[]{:S(2)}) %collective-permute-start.4) | collective-permute-done | bytes 262176 | tf_op jit(solution)/shard_map/ppermute | solution.py:11
  328.0 224.5 %collective-permute-done.5 = bf16[4,32,1024]{2,1,0:T(8,128)(2,1)S(1)} collective-permute-done((bf16[4,32,1024]{2,1,0:T(8,128)(2,1)}, bf16[4,32,1024]{2,1,0:T(8,128)(2,1)S(1)}, u32[]{:S(2)}, u32[]{:S(2)}) %collective-permute-start.5) | collective-permute-done | bytes 262176 | tf_op jit(solution)/shard_map/ppermute | solution.py:11
  552.5 54.5 %conditional.18 = (bf16[4,32,4096]{2,1,0:T(8,128)(2,1)}) conditional(s32[]{:T(128)} %convert_element_type.215, bf16[4,32,4096]{2,1,0:T(8,128)(2,1)} %get-tuple-element.1443, (pred[4,32,1024]{2,1,0:T(8,128)(4,1)S(1)}, bf16[4,32,1024]{2,1,0:T(8,128)(2,1)S(1)}, bf16[4,32,1024]{2,1,0:T(8,128)(2,1)S(1)}, s32[]{:T(128)}, f32[5,32,1024]{2,1,0:T(8,128)S(1)}, ...), branch_computations={%region_35.36_spmd, %region_36.39_spmd} | conditional | flops 270696448 | bytes 32834512 | solution.py:197
  552.5 11.7 %copy.25 = bf16[1024,4096]{1,0:T(8,128)(2,1)} copy(bf16[1024,4096]{0,1:T(8,128)(2,1)} %get-tuple-element.1582) | data formatting | bytes 16777216 | tf_op jit(solution)/shard_map
  565.4 41.5 %while.156 = (s32[]{:T(128)}, f32[32,1024]{1,0:T(8,128)}, f32[32,1024]{1,0:T(8,128)}, bf16[4,32,4096]{2,1,0:T(8,128)(2,1)}, bf16[4,32,1024]{2,1,0:T(8,128)(2,1)S...) while((s32[]{:T(128)}, f32[32,1024]{1,0:T(8,128)}, ...), condition=%wide.region_38.38_spmd, body=%wide.region_37.37_spmd.sunk | while | flops 270565376 | bytes 13042453 | solution.py:82
  566.5 1.8 multiply_multiply_fusion.8
  569.2 6.6 %fusion.206 = f32[32,1024]{1,0:T(8,128)} fusion(bf16[1024,4096]{1,0:T(8,128)(2,1)} %get-tuple-element.2378, f32[32,1024]{1,0:T(8,128)S(1)} %get-tuple-element.2227, f32[32,1024]{1,0:T(8,128)S(1)} %get-tuple-element.2229, f32[32,1024]{1,0:T(8,128)S(1)} %get-tuple-element.2230, f32[32,1024]{1,0:T(8,128)S(1)} %get-tuple-element.2231, f32[32]{0:T(128)S(1)} %fusion.205), kind=kOutput, calls=%fused_computation.162.clone.1 | convolution fusion | flops 269090816 | bytes 9044096 | tf_op jit(solution)/shard_map/cond/branch_1_fun/while/body/eval_jaxpr/dot_general | solution.py:46
  576.9 1.8 multiply_multiply_fusion.8
  579.5 6.6 %fusion.206 = f32[32,1024]{1,0:T(8,128)} fusion(bf16[1024,4096]{1,0:T(8,128)(2,1)} %get-tuple-element.2378, f32[32,1024]{1,0:T(8,128)S(1)} %get-tuple-element.2227, f32[32,1024]{1,0:T(8,128)S(1)} %get-tuple-element.2229, f32[32,1024]{1,0:T(8,128)S(1)} %get-tuple-element.2230, f32[32,1024]{1,0:T(8,128)S(1)} %get-tuple-element.2231, f32[32]{0:T(128)S(1)} %fusion.205), kind=kOutput, calls=%fused_computation.162.clone.1 | convolution fusion | flops 269090816 | bytes 9044096 | tf_op jit(solution)/shard_map/cond/branch_1_fun/while/body/eval_jaxpr/dot_general | solution.py:46
  587.3 1.8 multiply_multiply_fusion.8
  589.9 6.6 %fusion.206 = f32[32,1024]{1,0:T(8,128)} fusion(bf16[1024,4096]{1,0:T(8,128)(2,1)} %get-tuple-element.2378, f32[32,1024]{1,0:T(8,128)S(1)} %get-tuple-element.2227, f32[32,1024]{1,0:T(8,128)S(1)} %get-tuple-element.2229, f32[32,1024]{1,0:T(8,128)S(1)} %get-tuple-element.2230, f32[32,1024]{1,0:T(8,128)S(1)} %get-tuple-element.2231, f32[32]{0:T(128)S(1)} %fusion.205), kind=kOutput, calls=%fused_computation.162.clone.1 | convolution fusion | flops 269090816 | bytes 9044096 | tf_op jit(solution)/shard_map/cond/branch_1_fun/while/body/eval_jaxpr/dot_general | solution.py:46
  597.6 1.8 multiply_multiply_fusion.8
  600.3 6.6 %fusion.206 = f32[32,1024]{1,0:T(8,128)} fusion(bf16[1024,4096]{1,0:T(8,128)(2,1)} %get-tuple-element.2378, f32[32,1024]{1,0:T(8,128)S(1)} %get-tuple-element.2227, f32[32,1024]{1,0:T(8,128)S(1)} %get-tuple-element.2229, f32[32,1024]{1,0:T(8,128)S(1)} %get-tuple-element.2230, f32[32,1024]{1,0:T(8,128)S(1)} %get-tuple-element.2231, f32[32]{0:T(128)S(1)} %fusion.205), kind=kOutput, calls=%fused_computation.162.clone.1 | convolution fusion | flops 269090816 | bytes 9044096 | tf_op jit(solution)/shard_map/cond/branch_1_fun/while/body/eval_jaxpr/dot_general | solution.py:46
  606.9 1.6 copy.27
  608.9 18.6 %all_to_all.19 = bf16[128,8,512]{2,0,1:T(8,128)(2,1)S(1)} all-to-all(bf16[128,8,512]{2,0,1:T(8,128)(2,1)S(1)} %copy.26), channel_id=1, replica_groups=mesh['section'=4,'dp'=8] {'dp'}, dimensions={1} | all-to-all | bytes 2097152 | tf_op jit(solution)/shard_map/all_to_all | solution.py:206
  628.3 4.2 convolution_bitcast_fusion
  (87 shorter events, 40.9 us)
Async XLA Ops:
  8.0 3.4 copy-start
  8.0 28.3 %reduce-scatter.2.cloned.1.call-start = ((), (), s32[]{:S(2)}) async-start(), calls=%async_computation.2 | async-start | bytes 655360 | tf_op jit(solution)/shard_map/reduce_scatter | solution.py:110
  10.8 129.5 %all-gather.3.cloned.1.call-start = ((), (), s32[]{:S(2)}) async-start(), calls=%async_computation.3 | async-start | bytes 9437184 | tf_op jit(solution)/shard_map/all_gather | solution.py:116
  11.4 616.9 %all-gather.5.cloned.1.call-start = ((), (), s32[]{:S(2)}) async-start(), calls=%async_computation.4 | async-start | bytes 2359296 | tf_op jit(solution)/shard_map/all_gather | solution.py:208
  37.2 114.6 %copy-start.2 = (f32[1,4096]{1,0:T(1,128)S(1)}, f32[1,4096]{1,0:T(1,128)}, u32[]{:S(2)}) copy-start(f32[1,4096]{1,0:T(1,128)} %param.50) | copy-start | bytes 49156
  197.7 2.6 collective-permute-start
  200.4 50.3 %collective-permute-start.1 = (bf16[4,32,1024]{2,1,0:T(8,128)(2,1)S(1)}, bf16[4,32,1024]{2,1,0:T(8,128)(2,1)S(1)}, u32[]{:S(2)}, u32[]{:S(2)}) collective-permute-start(bf16[4,32,1024]{2,1,0:T(8,128)(2,1)S(1)} %get-tuple-element.1425), channel_id=1, source_target_pairs={{0,8},{8,16},{16,24},{1,9},{9,17},{17,25},{2,10},{10,18},{18,26},{... | collective-permute-start | bytes 786440 | tf_op jit(solution)/shard_map/ppermute | solution.py:11
  250.7 5.2 collective-permute-start.2
  255.9 1.8 copy-start.3
  255.9 1.8 copy-start.4
  256.9 2.0 copy-start.1
  262.0 54.6 %collective-permute-start.3 = (bf16[4,32,1024]{2,1,0:T(8,128)(2,1)}, bf16[4,32,1024]{2,1,0:T(8,128)(2,1)S(1)}, u32[]{:S(2)}, u32[]{:S(2)}) collective-permute-start(bf16[4,32,1024]{2,1,0:T(8,128)(2,1)} %get-tuple-element.1438), channel_id=1, source_target_pairs={{8,0},{16,8},{24,16},{9,1},{17,9},{25,17},{10,2},{18,10},{26,18},{... | collective-permute-start | bytes 786440 | tf_op jit(solution)/shard_map/ppermute | solution.py:11
  317.4 8.6 %collective-permute-start.4 = (bf16[4,32,1024]{2,1,0:T(8,128)(2,1)}, bf16[4,32,1024]{2,1,0:T(8,128)(2,1)S(1)}, u32[]{:S(2)}, u32[]{:S(2)}) collective-permute-start(bf16[4,32,1024]{2,1,0:T(8,128)(2,1)} %get-tuple-element.1442), channel_id=1, source_target_pairs={{8,0},{16,8},{24,16},{9,1},{17,9},{25,17},{10,2},{18,10},{26,18},{... | collective-permute-start | bytes 786440 | tf_op jit(solution)/shard_map/ppermute | solution.py:11
  326.7 225.7 %collective-permute-start.5 = (bf16[4,32,1024]{2,1,0:T(8,128)(2,1)}, bf16[4,32,1024]{2,1,0:T(8,128)(2,1)S(1)}, u32[]{:S(2)}, u32[]{:S(2)}) collective-permute-start(bf16[4,32,1024]{2,1,0:T(8,128)(2,1)} %get-tuple-element.1444), channel_id=1, source_target_pairs={{8,0},{16,8},{24,16},{9,1},{17,9},{25,17},{10,2},{18,10},{26,18},{... | collective-permute-start | bytes 786440 | tf_op jit(solution)/shard_map/ppermute | solution.py:11
Sparse Core Ops, SparseCore 0:
  11.9 24.3 reduce-scatter.1
Sparse Core Ops, SparseCore 1:
  13.4 126.9 all-gather.2
  257.8 140.8 all-gather.4
